TPU v7x, 8 devices: a whole 2x2x1 slice. The times are simulated.
8 devices in a mesh: replica: 1 (over z), pool: 8 (over y, x, core).
Axes of the slice: x: 2, y: 2, z: 1, core: 2. Of those that a mesh axis runs over, the one named last changes fastest.
Arguments:
- kv_pool: bfloat16 [2, 512, 2, 64, 8, 128], P(None, ('replica', 'pool'))
- page_idx: int32 [8, 8, 32], P(('replica', 'pool'))
- hidden: bfloat16 [8, 5120], P(('replica', 'pool'))
- norm_attn: bfloat16 [2, 5120], replicated
- norm_mlp: bfloat16 [2, 5120], replicated
- w_qkv: bfloat16 [2, 5120, 7168], replicated
- w_out: bfloat16 [2, 5120, 5120], replicated
- w_gate_up: bfloat16 [2, 5120, 27648], replicated
- w_down: bfloat16 [2, 13824, 5120], replicated
Outputs:
- output: bfloat16 [8, 5120], P(('replica', 'pool'))
All inputs are finite; a program needn't handle non-finite values.
Results may differ from a plain program's by a relative error of at most 0.0179669.
Values are sent between devices in bfloat16 or wider.
A program may use at most 4.25 GiB of HBM per device.

v0:
```python
import jax
import jax.numpy as jnp
from jax import lax
from jax.sharding import PartitionSpec as P

NORM_EPS = 1e-5
ROPE_BASE = 500000.0


def rms_norm(vec, gain):
    vec32 = vec.astype(jnp.float32)
    inv_rms = lax.rsqrt(jnp.mean(vec32 * vec32, axis=-1, keepdims=True) + NORM_EPS)
    return (vec32 * inv_rms * gain.astype(jnp.float32)).astype(jnp.bfloat16)


def rotary(heads_vec, position):
    head_dim = heads_vec.shape[-1]
    half_dim = head_dim // 2
    inv_freq = ROPE_BASE ** (-jnp.arange(half_dim, dtype=jnp.float32) * 2.0 / head_dim)
    angle = position * inv_freq
    cos_part = jnp.cos(angle)
    sin_part = jnp.sin(angle)
    vec32 = heads_vec.astype(jnp.float32)
    first = vec32[..., :half_dim]
    second = vec32[..., half_dim:]
    return jnp.concatenate([first * cos_part - second * sin_part, second * cos_part + first * sin_part], axis=-1).astype(jnp.bfloat16)


def project_qkv(hidden, gain, w_qkv, kv_heads, head_dim, position):
    row_count = hidden.shape[0]
    kv_width = kv_heads * head_dim
    q_width = w_qkv.shape[1] - 2 * kv_width
    qkv_rows = jnp.dot(rms_norm(hidden, gain), w_qkv, preferred_element_type=jnp.float32).astype(jnp.bfloat16)
    queries = rotary(qkv_rows[:, :q_width].reshape(row_count, kv_heads, q_width // head_dim // kv_heads, head_dim), position)
    key_new = rotary(qkv_rows[:, q_width:q_width + kv_width].reshape(row_count, kv_heads, head_dim), position)
    val_new = qkv_rows[:, q_width + kv_width:].reshape(row_count, kv_heads, head_dim)
    return queries, key_new, val_new


def attend(queries, key_new, val_new, keys_pre, vals_pre):
    score_scale = queries.shape[-1] ** -0.5
    scores_pre = jnp.einsum('bgrd,bngd->bgrn', queries, keys_pre, preferred_element_type=jnp.float32) * score_scale
    scores_new = jnp.einsum('bgrd,bgd->bgr', queries, key_new, preferred_element_type=jnp.float32) * score_scale
    score_max = jnp.maximum(jnp.max(scores_pre, axis=-1), scores_new)
    exp_pre = jnp.exp(scores_pre - score_max[..., None])
    exp_new = jnp.exp(scores_new - score_max)
    denominator = jnp.sum(exp_pre, axis=-1) + exp_new
    prob_pre = (exp_pre / denominator[..., None]).astype(jnp.bfloat16)
    prob_new = (exp_new / denominator).astype(jnp.bfloat16)
    mixed = jnp.einsum('bgrn,bngd->bgrd', prob_pre, vals_pre, preferred_element_type=jnp.float32)
    mixed = mixed + prob_new.astype(jnp.float32)[..., None] * val_new.astype(jnp.float32)[:, :, None, :]
    return mixed.astype(jnp.bfloat16).reshape(queries.shape[0], -1)


def finish_layer(hidden, attn_out, gain_mlp, w_out, w_gate_up, w_down):
    ffn_width = w_down.shape[0]
    attn_proj = jnp.dot(attn_out, w_out, preferred_element_type=jnp.float32)
    hidden_mid = (hidden.astype(jnp.float32) + attn_proj).astype(jnp.bfloat16)
    gate_up = jnp.dot(rms_norm(hidden_mid, gain_mlp), w_gate_up, preferred_element_type=jnp.float32).astype(jnp.bfloat16)
    ffn_act = (jax.nn.silu(gate_up[:, :ffn_width].astype(jnp.float32)) * gate_up[:, ffn_width:].astype(jnp.float32)).astype(jnp.bfloat16)
    ffn_out = jnp.dot(ffn_act, w_down, preferred_element_type=jnp.float32)
    return (hidden_mid.astype(jnp.float32) + ffn_out).astype(jnp.bfloat16)


def solution(mesh):
    def device_fn(kv_pool, page_idx, hidden, norm_attn, norm_mlp, w_qkv, w_out, w_gate_up, w_down):
        page_len = kv_pool.shape[3]
        kv_heads = kv_pool.shape[4]
        head_dim = kv_pool.shape[5]
        group_size = page_idx.shape[1]
        take_pages = page_idx.shape[2]
        prefix_len = group_size * take_pages * page_len
        position = float(prefix_len)
        wanted = lax.all_to_all(page_idx, 'pool', 1, 0, tiled=True).reshape(group_size * take_pages)
        for layer in range(kv_pool.shape[0]):
            queries, key_new, val_new = project_qkv(hidden, norm_attn[layer], w_qkv[layer], kv_heads, head_dim, position)
            outgoing = jnp.take(kv_pool[layer], wanted, axis=0).reshape(group_size, take_pages, 2, page_len, kv_heads, head_dim)
            received = lax.all_to_all(outgoing, 'pool', 0, 0, tiled=True)
            keys_pre = received[:, :, 0].reshape(1, prefix_len, kv_heads, head_dim)
            vals_pre = received[:, :, 1].reshape(1, prefix_len, kv_heads, head_dim)
            attn_out = attend(queries, key_new, val_new, keys_pre, vals_pre)
            hidden = finish_layer(hidden, attn_out, norm_mlp[layer], w_out[layer], w_gate_up[layer], w_down[layer])
        return hidden

    row_spec = P(('replica', 'pool'))
    in_specs = (P(None, ('replica', 'pool')), row_spec, row_spec, P(), P(), P(), P(), P(), P())
    return jax.shard_map(device_fn, mesh=mesh, in_specs=in_specs, out_specs=row_spec, check_vma=False)
```

profile of v0, /device:TPU:0, one launch (start us, length us, event | category | flops | bytes accessed | tf_op | source)
XLA Modules:
  0.0 1949.7 jit_solution(17527307948359359462)
XLA Ops:
  0.0 4.3 all-to-all-start
  4.3 23.0 %slice_bitcast_fusion = (bf16[64,2,64,8,128]{4,3,2,1,0:T(8,128)(2,1)}, bf16[64,2,64,8,128]{4,3,2,1,0:T(8,128)(2,1)}) fusion(bf16[2,64,2,64,8,128]{5,4,3,2,1,0:T(8,128)(2,1)} %param.11), kind=kLoop, calls=%fused_computation.30 | loop fusion | bytes 67108864 | tf_op jit(solution)/shard_map/squeeze | solution.py:77
  27.3 0.0 all-to-all-done
  27.3 0.5 broadcast.164
  27.9 0.7 reduce.23
  28.5 0.1 reshape.373
  28.6 29.2 %gather_fusion.1 = bf16[256,2,64,8,128]{4,3,2,1,0:T(8,128)(2,1)} fusion(bf16[64,2,64,8,128]{4,3,2,1,0:T(8,128)(2,1)} %get-tuple-element.10, s32[1024]{0:T(1024)S(1)} %pad_clamp_fusion), kind=kCustom, calls=%fused_computation.1.clone | custom fusion | bytes 134218752 | tf_op jit(solution)/shard_map/jit(_take)/gather | solution.py:77
  57.9 29.3 %gather_fusion = bf16[256,2,64,8,128]{4,3,2,1,0:T(8,128)(2,1)} fusion(bf16[64,2,64,8,128]{4,3,2,1,0:T(8,128)(2,1)} %get-tuple-element.11, s32[1024]{0:T(1024)S(1)} %pad_clamp_fusion), kind=kCustom, calls=%fused_computation.clone | custom fusion | bytes 134218752 | tf_op jit(solution)/shard_map/jit(_take)/gather | solution.py:77
  87.2 86.0 %broadcast_select_fusion = (bf16[256,2,64,8,128]{4,3,2,1,0:T(8,128)(2,1)}, bf16[256,2,64,8,128]{4,3,2,1,0:T(8,128)(2,1)}) fusion(bf16[256,2,64,8,128]{4,3,2,1,0:T(8,128)(2,1)} %gather_fusion.1, pred[256]{0:T(512)(128)(4,1)S(1)} %compare_and_fusion, bf16[256,2,64,8,128]{4,3,2,1,0:T(8,128)(2,1)} %gather_fusion), kind=kLoop, calls=%fused_computation.20 | loop fusion | flops 67108864 | bytes 268435712 | tf_op jit(solution)/shard_map/jit(_take)/select_n | solution.py:77
  173.2 44.7 %copy.20 = bf16[8,32,2,64,8,128]{5,3,1,4,2,0:T(8,128)(2,1)} copy(bf16[8,32,2,64,8,128]{5,4,3,2,1,0:T(8,128)(2,1)} %bitcast.6) | data formatting | bytes 134217728 | tf_op jit(solution)/shard_map/reshape | solution.py:77
  217.9 8.6 all-to-all-start.1
  226.4 44.6 %copy.23 = bf16[8,32,2,64,8,128]{5,3,1,4,2,0:T(8,128)(2,1)} copy(bf16[8,32,2,64,8,128]{5,4,3,2,1,0:T(8,128)(2,1)} %bitcast.27) | data formatting | bytes 134217728 | tf_op jit(solution)/shard_map/reshape | solution.py:77
  271.1 0.0 copy-start
  271.1 0.0 copy-start.1
  271.1 679.1 %all-to-all-done.1 = bf16[8,32,2,64,8,128]{5,3,1,4,2,0:T(8,128)(2,1)} async-done(((bf16[8,32,2,64,8,128]{5,3,1,4,2,0:T(8,128)(2,1)}), bf16[8,32,2,64,8,128]{5,3,1,4,2,0:T(8,128)(2,1)}, u32[]{:S(2)}, u32[]{:S(2)}) %all-to-all-start.1) | async-done | bytes 67108896 | tf_op jit(solution)/shard_map/all_to_all | solution.py:78
  950.2 8.7 all-to-all-start.2
  959.0 0.0 copy-done
  959.0 0.6 multiply_reduce_fusion.3
  960.3 0.0 copy-done.1
  960.3 24.6 %fusion.14 = f32[1,7168]{1,0:T(1,128)S(1)} fusion(bf16[2,5120,7168]{2,1,0:T(8,128)(2,1)} %param.16, bf16[2,5120]{1,0:T(2,128)(2,1)S(1)} %copy-done.1, bf16[1,5120]{1,0:T(2,128)(2,1)S(1)} %copy-done, f32[]{:T(128)S(6)} %rsqrt.16), kind=kOutput, calls=%fused_computation.16 | convolution fusion | flops 73425920 | bytes 73459712 | tf_op jit(solution)/shard_map/dot_general | solution.py:33
  985.0 0.1 fusion.84
  985.1 0.0 copy-start.5
  985.1 0.0 copy-start.7
  985.1 0.1 fusion.122
  985.2 0.1 maximum_bitcast_fusion
  985.3 0.1 fusion.110
  985.4 0.3 copy-done.5
  985.7 0.0 copy-done.7
  985.7 0.2 fusion.120
  985.9 43.3 %fusion.139 = (bf16[8,32,1,64,8,128]{5,3,1,4,2,0:T(8,128)(2,1)}, bf16[8,32,1,64,8,128]{5,3,1,4,2,0:T(8,128)(2,1)}) fusion(bf16[8,32,2,64,8,128]{5,3,1,4,2,0:T(8,128)(2,1)} %all-to-all-done.1), kind=kLoop, calls=%fused_computation.165 | loop fusion | bytes 134217728 | tf_op jit(solution)/shard_map/slice | solution.py:79
  1029.2 22.7 %copy.22 = bf16[8,32,1,64,8,128]{5,3,1,0,4,2:T(8,128)(2,1)} copy(bf16[8,32,1,64,8,128]{5,3,1,4,2,0:T(8,128)(2,1)} %get-tuple-element.9) | data formatting | bytes 67108864 | tf_op jit(solution)/shard_map/slice | solution.py:80
  1051.8 22.7 %copy.21 = bf16[8,32,1,64,8,128]{5,3,1,0,4,2:T(8,128)(2,1)} copy(bf16[8,32,1,64,8,128]{5,3,1,4,2,0:T(8,128)(2,1)} %get-tuple-element.8) | data formatting | bytes 67108864 | tf_op jit(solution)/shard_map/slice | solution.py:79
  1074.5 14.7 fusion.140
  1089.3 0.9 fusion.57
  1090.2 12.5 fusion.67
  1102.7 0.0 copy-start.3
  1102.7 18.6 multiply_reduce_fusion.2
  1122.0 0.0 copy-done.3
  1122.0 84.9 %fusion.2 = f32[1,27648]{1,0:T(1,128)S(1)} fusion(bf16[2,5120,27648]{2,1,0:T(8,128)(2,1)} %param.18, bf16[2,5120]{1,0:T(2,128)(2,1)S(1)} %copy-done.3, f32[1,5120]{1,0:T(1,128)S(1)} %get-tuple-element.33, f32[]{:T(128)S(6)} %rsqrt.17), kind=kOutput, calls=%fused_computation.4 | convolution fusion | flops 283136000 | bytes 283267072 | tf_op jit(solution)/shard_map/dot_general | solution.py:59
  1207.0 0.1 convert_element_type.248
  1207.0 0.0 copy-start.2
  1207.0 44.8 %multiply_reduce_fusion.1 = (f32[]{:T(128)}, f32[1,5120]{1,0:T(1,128)S(1)}) fusion(f32[1,5120]{1,0:T(1,128)S(1)} %get-tuple-element.33, bf16[2,13824,5120]{2,1,0:T(8,128)(2,1)} %param.19, bf16[1,27648]{1,0:T(2,128)(2,1)S(1)} %convert_element_type.248), kind=kOutput, calls=%fused_computation.100 | convolution fusion | flops 141693952 | bytes 141654016 | tf_op jit(solution)/shard_map/dot_general | solution.py:61
  1252.6 0.0 copy-done.2
  1252.6 24.6 %fusion.12 = f32[1,7168]{1,0:T(1,128)S(1)} fusion(bf16[2,5120,7168]{2,1,0:T(8,128)(2,1)} %param.16, bf16[2,5120]{1,0:T(2,128)(2,1)S(1)} %copy-done.2, f32[1,5120]{1,0:T(1,128)S(1)} %get-tuple-element.35, f32[]{:T(128)S(6)} %rsqrt.18), kind=kOutput, calls=%fused_computation.14 | convolution fusion | flops 73420800 | bytes 73469952 | tf_op jit(solution)/shard_map/dot_general | solution.py:33
  1277.2 0.1 fusion.83
  1277.3 405.3 %all-to-all-done.2 = bf16[8,32,2,64,8,128]{5,3,1,4,2,0:T(8,128)(2,1)} async-done(((bf16[8,32,2,64,8,128]{5,3,1,4,2,0:T(8,128)(2,1)}), bf16[8,32,2,64,8,128]{5,3,1,4,2,0:T(8,128)(2,1)}, u32[]{:S(2)}, u32[]{:S(2)}) %all-to-all-start.2) | async-done | bytes 67108896 | tf_op jit(solution)/shard_map/all_to_all | solution.py:78
  1682.6 44.0 %fusion.138 = (bf16[8,32,1,64,8,128]{5,3,1,4,2,0:T(8,128)(2,1)}, bf16[8,32,1,64,8,128]{5,3,1,4,2,0:T(8,128)(2,1)}) fusion(bf16[8,32,2,64,8,128]{5,3,1,4,2,0:T(8,128)(2,1)} %all-to-all-done.2), kind=kLoop, calls=%fused_computation.164 | loop fusion | bytes 134217728 | tf_op jit(solution)/shard_map/slice | solution.py:79
  1726.6 22.6 %copy.25 = bf16[8,32,1,64,8,128]{5,3,1,0,4,2:T(8,128)(2,1)} copy(bf16[8,32,1,64,8,128]{5,3,1,4,2,0:T(8,128)(2,1)} %get-tuple-element.7) | data formatting | bytes 67108864 | tf_op jit(solution)/shard_map/slice | solution.py:80
  1749.2 22.6 %copy.24 = bf16[8,32,1,64,8,128]{5,3,1,0,4,2:T(8,128)(2,1)} copy(bf16[8,32,1,64,8,128]{5,3,1,4,2,0:T(8,128)(2,1)} %get-tuple-element.6) | data formatting | bytes 67108864 | tf_op jit(solution)/shard_map/slice | solution.py:79
  1771.9 0.0 copy-done.6
  1771.9 0.0 copy-done.8
  1771.9 0.1 fusion.112
  1772.0 0.1 fusion.125
  1772.1 0.1 maximum_bitcast_fusion.1
  1772.1 14.7 fusion.141
  1786.9 0.2 fusion.118
  1787.1 0.9 fusion.58
  1788.0 12.5 fusion.68
  1800.5 0.0 copy-start.4
  1800.5 18.9 multiply_reduce_fusion
  1820.1 0.0 copy-done.4
  1820.1 85.2 %fusion = f32[1,27648]{1,0:T(1,128)S(1)} fusion(bf16[2,5120,27648]{2,1,0:T(8,128)(2,1)} %param.18, bf16[2,5120]{1,0:T(2,128)(2,1)S(1)} %copy-done.4, f32[1,5120]{1,0:T(1,128)S(1)} %get-tuple-element.39, f32[]{:T(128)S(6)} %rsqrt.19), kind=kOutput, calls=%fused_computation.2 | convolution fusion | flops 283136000 | bytes 283267072 | tf_op jit(solution)/shard_map/dot_general | solution.py:59
  1905.3 0.1 convert_element_type.273
  1905.3 44.3 %fusion.54 = bf16[1,5120]{1,0:T(2,128)(2,1)} fusion(f32[1,5120]{1,0:T(1,128)S(1)} %get-tuple-element.39, bf16[2,13824,5120]{2,1,0:T(8,128)(2,1)} %param.19, bf16[1,27648]{1,0:T(2,128)(2,1)S(1)} %convert_element_type.273), kind=kOutput, calls=%fused_computation.42 | convolution fusion | flops 141678592 | bytes 141643776 | tf_op jit(solution)/shard_map/dot_general | solution.py:61
  (22 shorter events, 0.2 us)
Async XLA Ops:
  0.0 27.3 %all-to-all-start = ((s32[1,8,32]{2,0,1:T(1,128)}), s32[1,8,32]{2,0,1:T(1,128)S(1)}, u32[]{:S(2)}, u32[]{:S(2)}) async-start(s32[1,8,32]{2,0,1:T(1,128)} %bitcast.154), calls=%async_computation | async-start | bytes 8192 | tf_op jit(solution)/shard_map/all_to_all | solution.py:74
  217.9 732.3 %all-to-all-start.1 = ((bf16[8,32,2,64,8,128]{5,3,1,4,2,0:T(8,128)(2,1)}), bf16[8,32,2,64,8,128]{5,3,1,4,2,0:T(8,128)(2,1)}, u32[]{:S(2)}, u32[]{:S(2)}) async-start(bf16[8,32,2,64,8,128]{5,3,1,4,2,0:T(8,128)(2,1)} %copy.20), calls=%async_computation.1 | async-start | bytes 134217728 | tf_op jit(solution)/shard_map/all_to_all | solution.py:78
  271.1 687.9 %copy-start = (bf16[1,5120]{1,0:T(2,128)(2,1)S(1)}, bf16[1,5120]{1,0:T(2,128)(2,1)}, u32[]{:S(2)}) copy-start(bf16[1,5120]{1,0:T(2,128)(2,1)} %param.13) | copy-start | bytes 30724
  271.1 689.2 %copy-start.1 = (bf16[2,5120]{1,0:T(2,128)(2,1)S(1)}, bf16[2,5120]{1,0:T(2,128)(2,1)}, u32[]{:S(2)}) copy-start(bf16[2,5120]{1,0:T(2,128)(2,1)} %param.14) | copy-start | bytes 61444
  950.2 732.3 %all-to-all-start.2 = ((bf16[8,32,2,64,8,128]{5,3,1,4,2,0:T(8,128)(2,1)}), bf16[8,32,2,64,8,128]{5,3,1,4,2,0:T(8,128)(2,1)}, u32[]{:S(2)}, u32[]{:S(2)}) async-start(bf16[8,32,2,64,8,128]{5,3,1,4,2,0:T(8,128)(2,1)} %copy.23), calls=%async_computation.2 | async-start | bytes 134217728 | tf_op jit(solution)/shard_map/all_to_all | solution.py:78
  985.1 0.6 copy-start.5
  985.1 0.6 copy-start.7
  1102.7 19.3 copy-start.3
  1207.0 45.5 %copy-start.2 = (bf16[2,5120]{1,0:T(2,128)(2,1)S(1)}, bf16[2,5120]{1,0:T(2,128)(2,1)}, u32[]{:S(2)}) copy-start(bf16[2,5120]{1,0:T(2,128)(2,1)} %param.14) | copy-start | bytes 61444
  1749.2 22.6 %copy-start.6 = (f32[64]{0:T(128)S(1)}, f32[64]{0:T(128)}, u32[]{:S(2)}) copy-start(f32[64]{0:T(128)} %copy-done.5) | copy-start | bytes 772
  1749.2 22.6 %copy-start.8 = (f32[64]{0:T(128)S(1)}, f32[64]{0:T(128)}, u32[]{:S(2)}) copy-start(f32[64]{0:T(128)} %copy-done.7) | copy-start | bytes 772
  1800.5 19.6 %copy-start.4 = (bf16[2,5120]{1,0:T(2,128)(2,1)S(1)}, bf16[2,5120]{1,0:T(2,128)(2,1)}, u32[]{:S(2)}) copy-start(bf16[2,5120]{1,0:T(2,128)(2,1)} %param.15) | copy-start | bytes 61444
where the time goes:
time: 1950 us
  waiting for transfers between devices  1080 us (55%)
  matrix products  401 us (21%)
  local copies, waits for them, and re-layouts  350 us (18%)
  other arithmetic  89.8 us (5%)
  starting transfers between devices  21.6 us (1%)
    all_to_all x2, waiting for transfers between devices, device_fn(): received = lax.all_to_all(outgoing, 'pool', 0, 0, tiled=True)  1080 us
    dot_general x2, matrix products, finish_layer(): jnp.dot(rms_norm(hidden_mid, gain_mlp), w_gate_up, preferred_element_type...  170 us
    slice x4, local copies, waits for them, and re-layouts, device_fn(): keys_pre = received[:, :, 0].reshape(1, prefix_len, kv_heads, head_dim)  133 us
    reshape x2, local copies, waits for them, and re-layouts, device_fn(): jnp.take(kv_pool[layer], wanted, axis=0)  89.3 us
    dot_general x2, matrix products, finish_layer(): ffn_out = jnp.dot(ffn_act, w_down, preferred_element_type=jnp.float32)  89.1 us
    select_n x2, other arithmetic, device_fn(): jnp.take(kv_pool[layer], wanted, axis=0)  86 us
    gather x2, local copies, waits for them, and re-layouts, device_fn(): jnp.take(kv_pool[layer], wanted, axis=0)  58.5 us
    dot_general x2, matrix products, project_qkv(): jnp.dot(rms_norm(hidden, gain), w_qkv, preferred_element_type=jnp.float32)  49.2 us
  transfers between devices with their start and end apart: 3, of which 2 were waited for; matrix products, arithmetic and copies ran while one was open for 20% of the time, Pallas kernels for 0%

commit v1 on v0

v1 whole, which is shorter than its diff:
```python
import functools
import math

import jax
import jax.numpy as jnp
import numpy as np
from jax import lax
from jax.experimental import pallas as pl
from jax.experimental.pallas import tpu as pltpu
from jax.sharding import PartitionSpec as P

NORM_EPS = 1e-5
ROPE_BASE = 500000.0
NEG = -3.0e38
MESH = pl.DeviceIdType.MESH
F32 = jnp.float32
BF16 = jnp.bfloat16

N_DEV = 8
GU_SLOTS = 3
DN_SLOTS = 4
STEP = 256
PAGES_PER_ITER = 16


def rope_table(position, head_dim):
    half = head_dim // 2
    freq = ROPE_BASE ** (-np.arange(half, dtype=np.float64) * 2.0 / head_dim)
    angle = position * freq
    cos = np.concatenate([np.cos(angle), np.cos(angle)])
    sin = np.concatenate([-np.sin(angle), np.sin(angle)])
    return np.stack([cos, sin]).astype(np.float32)


def kernel(dims, kv, pidx, hid, na, nm, rope, wqkv, wout, wgu, wdn, o,
           wq_b, k_b, v_b, wo_b, gu_b, dn_b, s_b,
           hid_v, na_v, nm_v, pidx_v, rope_v, x0, xf, xm, qbuf, psend, precv,
           abuf, mbuf, msend, mrecv, maskx, mrow, snew, vnew_b,
           sm_sem, wq_sem, k_sem, v_sem, wo_sem, gu_sem, dn_sem,
           x0_s, x0_r, mk_s, mk_r, q_s, q_r, p_s, p_r, a_s, a_r, xm_s, xm_r, xf_s, xf_r, m_s, m_r):
    layers, pages, page_len, kv_heads, head_dim, rep_q, width, ffn, steps = dims
    pairs = kv_heads // 2
    slice_w = width // N_DEV
    q_w = rep_q * head_dim
    rows = rep_q * N_DEV
    scale2 = float(head_dim ** -0.5 * math.log2(math.e))

    me = lax.axis_index('pool')
    rep = lax.axis_index('replica')
    b0 = lax.rem(me, 2)
    b1 = lax.rem(me // 2, 2)
    b2 = me // 4

    def peer(k):
        return lax.rem(b0 + k % 2, 2) + 2 * lax.rem(b1 + (k // 2) % 2, 2) + 4 * lax.rem(b2 + k // 4, 2)

    def pair_of(kx):
        return lax.rem(b1 + kx % 2, 2) + 2 * lax.rem(b2 + kx // 2, 2)

    def remote(src, dst, ssem, rsem, k):
        return pltpu.make_async_remote_copy(src_ref=src, dst_ref=dst, send_sem=ssem, recv_sem=rsem,
                                            device_id=(rep, peer(k)), device_id_type=MESH)

    FAR_FIRST = (6, 7, 4, 5, 2, 3, 1)

    def my_cols(ref, w):
        return ref.at[:, pl.ds(pl.multiple_of(me * w, 128), w)]

    def wq_copies(l):
        out = []
        base = 0
        for i, (off, w) in enumerate(((0, q_w), (width, head_dim), (width + kv_heads * head_dim, head_dim))):
            src = wqkv.at[l, :, pl.ds(pl.multiple_of(off + me * w, 128), w)]
            out.append(pltpu.make_async_copy(src, wq_b.at[:, pl.ds(base, w)], wq_sem.at[i]))
            base += w
        return out

    def kv_copies(l, which, buf, sem):
        return [pltpu.make_async_copy(kv.at[l, :, which, :, p], buf.at[p], sem.at[p]) for p in range(pairs)]

    def wo_copy(l):
        return pltpu.make_async_copy(wout.at[l, :, pl.ds(pl.multiple_of(me * slice_w, 128), slice_w)], wo_b, wo_sem.at[0])

    def ffn_base(dev):
        return 128 * ((dev * (ffn // 128)) // N_DEV)

    def gu_copies(l, s):
        slot = lax.rem(l * steps + s, GU_SLOTS)
        return [pltpu.make_async_copy(
            wgu.at[l, :, pl.ds(pl.multiple_of(part * ffn + ffn_base(me) + s * STEP, 128), STEP)],
            gu_b.at[slot, part], gu_sem.at[slot, part]) for part in range(2)]

    def dn_copies(l, s):
        slot = lax.rem(l * steps + s, DN_SLOTS)
        return [pltpu.make_async_copy(
            wdn.at[l, pl.ds(pl.multiple_of(ffn_base(j) + s * STEP, 128), STEP),
                   pl.ds(pl.multiple_of(me * slice_w, 128), slice_w)],
            dn_b.at[slot, pl.ds(j * STEP, STEP)], dn_sem.at[slot, j]) for j in range(N_DEV)]

    def start(cps):
        for c in cps:
            c.start()

    def wait(cps):
        for c in cps:
            c.wait()

    small = [pltpu.make_async_copy(a, b, sm_sem.at[i]) for i, (a, b) in enumerate(
        ((hid, hid_v), (pidx.at[0], pidx_v), (na, na_v), (nm, nm_v), (rope, rope_v)))]
    start(small)
    start(wq_copies(0))
    start(kv_copies(0, 0, k_b, k_sem))

    barrier = pltpu.get_barrier_semaphore()
    for k in range(1, N_DEV):
        pl.semaphore_signal(barrier, inc=1, device_id=(rep, peer(k)), device_id_type=MESH)
    wait(small)
    x0[me] = hid_v[...].astype(F32)
    lane = lax.broadcasted_iota(jnp.int32, (N_DEV, 128), 1)
    idx = pidx_v[...]
    hit = lane < 0
    for j in range(idx.shape[1]):
        hit = jnp.logical_or(hit, idx[:, j:j + 1] == lane)
    hitf = jnp.where(hit, 1.0, 0.0).astype(F32)
    for owner in range(N_DEV):
        msend[owner] = jnp.broadcast_to(hitf[owner:owner + 1, :], (N_DEV, 128))
    pl.semaphore_wait(barrier, N_DEV - 1)
    x0_cps = [remote(x0.at[me], x0.at[me], x0_s.at[k], x0_r.at[k], k) for k in FAR_FIRST]
    start(x0_cps)
    mk_cps = [remote(msend.at[peer(k)], mrecv.at[me], mk_s.at[k], mk_r.at[k], k) for k in FAR_FIRST]
    start(mk_cps)
    mrecv[me] = msend[me]
    start(kv_copies(0, 1, v_b, v_sem))
    wait(x0_cps)
    sub8 = lax.broadcasted_iota(jnp.int32, (N_DEV, width), 0)
    xin = jnp.zeros((N_DEV, width), F32)
    for j in range(N_DEV):
        xin = jnp.where(sub8 == j, jnp.broadcast_to(x0[j], (N_DEV, width)), xin)
    xf[...] = xin.astype(BF16)

    odd = lax.rem(lax.broadcasted_iota(jnp.int32, (rows, 128), 1), 2) == 1
    grp = lax.broadcasted_iota(jnp.int32, (N_DEV, 128), 1) // 16
    low8 = lax.rem(lax.broadcasted_iota(jnp.int32, (N_DEV, 128), 1), 16) < 8

    def norm(x, gains, l):
        g = jnp.where(l == 0, gains[0:1, :].astype(F32), gains[1:2, :].astype(F32))
        inv = lax.rsqrt(jnp.sum(x * x, axis=-1, keepdims=True) / width + NORM_EPS)
        return (x * inv * g).astype(BF16)

    def layer(l, carry):
        h = norm(xf[...].astype(F32), na_v[...], l)
        wait(wq_copies(l))
        u = jnp.dot(h, wq_b[...], preferred_element_type=F32).astype(BF16).astype(F32)

        @pl.when(l == 0)
        def _():
            start([wo_copy(0)])
            for s in range(GU_SLOTS):
                start(gu_copies(0, s))
            for s in range(DN_SLOTS):
                start(dn_copies(0, s))

        @pl.when(l + 1 < layers)
        def _():
            start(wq_copies(l + 1))

        cos = rope_v[0:1, :]
        sin = rope_v[1:2, :]

        def rot(v):
            return (v * cos + pltpu.roll(v, head_dim // 2, 1) * sin).astype(BF16)

        qs = [rot(u[:, g * head_dim:(g + 1) * head_dim]).astype(F32) for g in range(rep_q)]
        kn = rot(u[:, q_w:q_w + head_dim]).astype(F32)
        vnew_b[...] = u[:, q_w + head_dim:]
        qbuf[me] = jnp.concatenate(qs, axis=0).astype(BF16)
        q_cps = {k: remote(qbuf.at[me], qbuf.at[me], q_s.at[k], q_r.at[k], k) for k in range(1, N_DEV)}
        start([q_cps[k] for k in FAR_FIRST])
        for g in range(rep_q):
            snew[g] = jnp.broadcast_to(jnp.sum(qs[g] * kn, axis=-1, keepdims=True), (N_DEV, 128))

        @pl.when(l == 0)
        def _():
            wait(mk_cps)
            sub = lax.broadcasted_iota(jnp.int32, (N_DEV, 128), 0)
            mk = jnp.zeros((N_DEV, 128), F32)
            for r in range(N_DEV):
                mk = jnp.where(sub == r, mrecv[r], mk)
            for p in range(pages):
                maskx[p] = jnp.broadcast_to(mk[:, p:p + 1], (N_DEV, 128))

        wait(kv_copies(l, 0, k_b, k_sem))
        flat = PAGES_PER_ITER * page_len * 2
        for kx in range(pairs):
            for k in (2 * kx, 2 * kx + 1):
                if k:
                    q_cps[k].wait()
            p = pair_of(kx)
            q2 = jnp.concatenate([qbuf[2 * p], qbuf[2 * p + 1]], axis=0)

            def score_body(c, mx, p=p, q2=q2, kx=kx):
                kt = k_b[p, pl.ds(c * PAGES_PER_ITER, PAGES_PER_ITER)].reshape(flat, head_dim)
                s = lax.dot_general(q2, kt, (((1,), (1,)), ((), ())), preferred_element_type=F32)
                for i in range(PAGES_PER_ITER):
                    cols = slice(i * 128, (i + 1) * 128)
                    keep = maskx[c * PAGES_PER_ITER + i] > 0.5
                    keep = jnp.concatenate([keep] * rep_q, axis=0)
                    sp = jnp.where(odd, s[rows:, cols], s[:rows, cols])
                    sp = jnp.where(keep, sp, NEG)
                    s_b[kx, c * PAGES_PER_ITER + i] = sp
                    mx = jnp.maximum(mx, sp)
                return mx

            mx = lax.fori_loop(0, pages // PAGES_PER_ITER, score_body, jnp.full((rows, 128), NEG, F32))
            m_e = jnp.max(jnp.where(odd, NEG, mx), axis=-1, keepdims=True)
            m_o = jnp.max(jnp.where(odd, mx, NEG), axis=-1, keepdims=True)
            mrow[kx] = jnp.where(odd, m_o, m_e)

        @pl.when(l + 1 < layers)
        def _():
            start(kv_copies(l + 1, 0, k_b, k_sem))

        wait(kv_copies(l, 1, v_b, v_sem))
        p_cps = {k: remote(psend.at[peer(k)], precv.at[me], p_s.at[k], p_r.at[k], k) for k in range(1, N_DEV)}
        for kx in reversed(range(pairs)):
            p = pair_of(kx)
            m = mrow[kx]

            def value_body(c, carry, p=p, m=m, kx=kx):
                acc, den = carry
                pieces = []
                for i in range(PAGES_PER_ITER):
                    e = jnp.exp2((s_b[kx, c * PAGES_PER_ITER + i] - m) * scale2)
                    den = den + e
                    pieces.append(jnp.concatenate([jnp.where(odd, 0.0, e), jnp.where(odd, e, 0.0)], axis=0).astype(BF16))
                vt = v_b[p, pl.ds(c * PAGES_PER_ITER, PAGES_PER_ITER)].reshape(flat, head_dim)
                acc = acc + jnp.dot(jnp.concatenate(pieces, axis=1), vt, preferred_element_type=F32)
                return acc, den

            acc, den = lax.fori_loop(0, pages // PAGES_PER_ITER, value_body,
                                     (jnp.zeros((2 * rows, head_dim), F32), jnp.zeros((rows, 128), F32)))
            for hh in range(2):
                par = odd if hh else jnp.logical_not(odd)
                l_h = jnp.sum(jnp.where(par, den, 0.0), axis=-1, keepdims=True)
                m_h = jnp.max(jnp.where(par, m, NEG), axis=-1, keepdims=True)
                stat = jnp.zeros((N_DEV, 128), F32)
                for g in range(rep_q):
                    rs = slice(g * N_DEV, (g + 1) * N_DEV)
                    psend[2 * p + hh, g] = acc[hh * rows + g * N_DEV:hh * rows + (g + 1) * N_DEV]
                    stat = jnp.where(grp == g, jnp.where(low8, m_h[rs], l_h[rs]), stat)
                psend[2 * p + hh, rep_q] = stat
            for k in (2 * kx, 2 * kx + 1):
                if k:
                    p_cps[k].start()
        precv[me] = psend[me]

        @pl.when(l + 1 < layers)
        def _():
            start(kv_copies(l + 1, 1, v_b, v_sem))

        wait([p_cps[k] for k in FAR_FIRST])
        stats = [precv[j, rep_q] for j in range(N_DEV)]
        heads_out = []
        for g in range(rep_q):
            ms = [jnp.broadcast_to(st[:, 16 * g:16 * g + 1], (N_DEV, 128)) for st in stats]
            ls = [jnp.broadcast_to(st[:, 16 * g + 8:16 * g + 9], (N_DEV, 128)) for st in stats]
            sn = snew[g]
            top = sn
            for mj in ms:
                top = jnp.maximum(top, mj)
            e_new = jnp.exp2((sn - top) * scale2)
            den = e_new
            num = jnp.zeros((N_DEV, head_dim), F32)
            for j in range(N_DEV):
                w = jnp.exp2((ms[j] - top) * scale2)
                den = den + w * ls[j]
                num = num + w * precv[j, g]
            p_new = (e_new / den).astype(BF16).astype(F32)
            heads_out.append(num / den + p_new * vnew_b[...])
        my_cols(abuf, q_w)[...] = jnp.concatenate(heads_out, axis=1).astype(BF16)
        a_cps = [remote(my_cols(abuf, q_w), my_cols(abuf, q_w), a_s.at[k], a_r.at[k], k) for k in FAR_FIRST]
        start(a_cps)
        wait([wo_copy(l)])
        wait(a_cps)

        proj = jnp.dot(abuf[...], wo_b[...], preferred_element_type=F32)
        my_cols(xm, slice_w)[...] = (my_cols(xf, slice_w)[...].astype(F32) + proj).astype(BF16)
        xm_cps = [remote(my_cols(xm, slice_w), my_cols(xm, slice_w), xm_s.at[k], xm_r.at[k], k) for k in FAR_FIRST]
        start(xm_cps)
        wait(xm_cps)

        h2 = norm(xm[...].astype(F32), nm_v[...], l)
        mlane = lax.broadcasted_iota(jnp.int32, (N_DEV, STEP), 1)

        def m_cps(s):
            cols = pl.ds(pl.multiple_of(me * STEP, 128), STEP)
            return [remote(mbuf.at[s, :, cols], mbuf.at[s, :, cols], m_s.at[s, k], m_r.at[s, k], k) for k in FAR_FIRST]

        def up_body(s, carry):
            slot = lax.rem(l * steps + s, GU_SLOTS)
            wait(gu_copies(l, s))
            gate = jnp.dot(h2, gu_b[slot, 0], preferred_element_type=F32).astype(BF16).astype(F32)
            up = jnp.dot(h2, gu_b[slot, 1], preferred_element_type=F32).astype(BF16).astype(F32)
            act = gate / (1.0 + jnp.exp(-gate)) * up
            dup = jnp.logical_and(jnp.logical_and(b0 == 1, s == 0), mlane < 128)
            act = jnp.where(dup, 0.0, act).astype(BF16)
            mbuf[s, :, pl.ds(pl.multiple_of(me * STEP, 128), STEP)] = act
            start(m_cps(s))

            @pl.when(s + GU_SLOTS < steps)
            def _():
                start(gu_copies(l, s + GU_SLOTS))
            return carry

        lax.fori_loop(0, steps, up_body, 0)

        def down_body(s, acc):
            slot = lax.rem(l * steps + s, DN_SLOTS)
            wait(dn_copies(l, s))
            wait(m_cps(s))
            acc = acc + jnp.dot(mbuf[s], dn_b[slot], preferred_element_type=F32)

            @pl.when(s + DN_SLOTS < steps)
            def _():
                start(dn_copies(l, s + DN_SLOTS))
            return acc

        acc = lax.fori_loop(0, steps, down_body, jnp.zeros((N_DEV, slice_w), F32))
        my_cols(xf, slice_w)[...] = (my_cols(xm, slice_w)[...].astype(F32) + acc).astype(BF16)
        xf_cps = [remote(my_cols(xf, slice_w), my_cols(xf, slice_w), xf_s.at[k], xf_r.at[k], k) for k in FAR_FIRST]
        start(xf_cps)

        @pl.when(l + 1 < layers)
        def _():
            start([wo_copy(l + 1)])
            for s in range(GU_SLOTS):
                start(gu_copies(l + 1, s))
            for s in range(DN_SLOTS):
                start(dn_copies(l + 1, s))

        wait(xf_cps)
        return carry

    lax.fori_loop(0, layers, layer, 0)
    xo = xf[...].astype(F32)
    o[...] = jnp.sum(jnp.where(sub8 == me, xo, 0.0), axis=0, keepdims=True).astype(BF16)


def solution(mesh):
    def device_fn(kv_pool, page_idx, hidden, norm_attn, norm_mlp, w_qkv, w_out, w_gate_up, w_down):
        layers, pages, _, page_len, kv_heads, head_dim = kv_pool.shape
        group, take = page_idx.shape[1:]
        width = hidden.shape[1]
        ffn = w_down.shape[1]
        rep_q = (w_qkv.shape[2] - 2 * kv_heads * head_dim) // head_dim // kv_heads
        rows = rep_q * group
        slice_w = width // group
        q_w = rep_q * head_dim
        steps = -(-(-(-(ffn // 128) // group)) // (STEP // 128))
        position = float(group * take * page_len)
        rope = jnp.asarray(rope_table(position, head_dim))
        kv = kv_pool.reshape(layers, pages, 2, page_len, kv_heads // 2, 2, head_dim)
        dims = (layers, pages, page_len, kv_heads, head_dim, rep_q, width, ffn, steps)
        dma = pltpu.SemaphoreType.DMA
        any_spec = pl.BlockSpec(memory_space=pl.ANY)
        pairs = kv_heads // 2
        return pl.pallas_call(
            functools.partial(kernel, dims),
            out_shape=jax.ShapeDtypeStruct((1, width), BF16),
            in_specs=[any_spec] * 10,
            out_specs=pl.BlockSpec(memory_space=pltpu.VMEM),
            scratch_shapes=[
                pltpu.VMEM((width, q_w + 2 * head_dim), BF16),
                pltpu.VMEM((pairs, pages, page_len, 2, head_dim), BF16),
                pltpu.VMEM((pairs, pages, page_len, 2, head_dim), BF16),
                pltpu.VMEM((width, slice_w), BF16),
                pltpu.VMEM((GU_SLOTS, 2, width, STEP), BF16),
                pltpu.VMEM((DN_SLOTS, group * STEP, slice_w), BF16),
                pltpu.VMEM((pairs, pages, rows, 128), F32),
                pltpu.VMEM((1, width), BF16),
                pltpu.VMEM((layers, width), BF16),
                pltpu.VMEM((layers, width), BF16),
                pltpu.VMEM((group, take), jnp.int32),
                pltpu.VMEM((2, head_dim), F32),
                pltpu.VMEM((group, 1, width), F32),
                pltpu.VMEM((group, width), BF16),
                pltpu.VMEM((group, width), BF16),
                pltpu.VMEM((group, rows, head_dim), BF16),
                pltpu.VMEM((group, rep_q + 1, group, 128), F32),
                pltpu.VMEM((group, rep_q + 1, group, 128), F32),
                pltpu.VMEM((group, width), BF16),
                pltpu.VMEM((steps, group, group * STEP), BF16),
                pltpu.VMEM((group, group, 128), F32),
                pltpu.VMEM((group, group, 128), F32),
                pltpu.VMEM((pages, group, 128), F32),
                pltpu.VMEM((pairs, rows, 128), F32),
                pltpu.VMEM((rep_q, group, 128), F32),
                pltpu.VMEM((group, head_dim), F32),
                dma((5,)), dma((3,)), dma((pairs,)), dma((pairs,)), dma((1,)),
                dma((GU_SLOTS, 2)), dma((DN_SLOTS, group)),
            ] + [dma((group,))] * 14 + [dma((steps, group))] * 2,
            compiler_params=pltpu.CompilerParams(
                collective_id=0, has_side_effects=True, vmem_limit_bytes=67_043_328),
            name="decode_step",
        )(kv, page_idx, hidden, norm_attn, norm_mlp, rope, w_qkv, w_out, w_gate_up, w_down)

    row_spec = P(('replica', 'pool'))
    in_specs = (P(None, ('replica', 'pool')), row_spec, row_spec, P(), P(), P(), P(), P(), P())
    return jax.shard_map(device_fn, mesh=mesh, in_specs=in_specs, out_specs=row_spec, check_vma=False)
```

time: 1950 us -> 98.1 us (0.05)
  waiting for transfers between devices: 1080 us -> 0 us
  matrix products: 401 us -> 0 us
  local copies, waits for them, and re-layouts: 350 us -> 1.36 us
  Pallas kernels: 0 us -> 96.5 us
  other arithmetic: 89.8 us -> 0 us
  starting transfers between devices: 21.6 us -> 0 us
    all_to_all x3 -> x0, waiting for transfers between devices: 1080 us -> none  [the longest x2 1080 us: device_fn(): received = lax.all_to_all(outgoing, 'pool', 0, 0, tiled=True)]
    dot_general x14 -> x0, matrix products: 401 us -> none  [the longest x2 170 us: finish_layer(): jnp.dot(rms_norm(hidden_mid, gain_mlp), w_gate_up, preferred_element_type...]
    slice x6 -> x0, local copies, waits for them, and re-layouts: 178 us -> none  [the longest x4 133 us: device_fn(): keys_pre = received[:, :, 0].reshape(1, prefix_len, kv_heads, head_dim)]
    pallas_call x0 -> x1, Pallas kernels: none -> 96.5 us  [device_fn(): pl.pallas_call(functools.partial(kernel, dims), out_shape=jax.ShapeDtypeS...]
    reshape x3 -> x0, local copies, waits for them, and re-layouts: 89.4 us -> none  [the longest x2 89.3 us: device_fn(): jnp.take(kv_pool[layer], wanted, axis=0)]
    select_n x2 -> x0, other arithmetic: 86 us -> none  [device_fn(): jnp.take(kv_pool[layer], wanted, axis=0)]
    gather x2 -> x0, local copies, waits for them, and re-layouts: 58.5 us -> none  [device_fn(): jnp.take(kv_pool[layer], wanted, axis=0)]
    squeeze x1 -> x0, local copies, waits for them, and re-layouts: 23 us -> none  [device_fn(): kv_pool[layer]]
  transfers between devices with their start and end apart: 3 -> 0, of which waited for: 2 -> 0; matrix products, arithmetic and copies ran while one was open for 20% -> 0% of each run, Pallas kernels for 0% -> 0%
where the time goes in v1:
time: 98.1 us; the launch traced here: 97.9 us
  Pallas kernels  96.5 us (98%)
  local copies, waits for them, and re-layouts  1.36 us (1%)
    pallas_call x1, Pallas kernels, device_fn(): pl.pallas_call(functools.partial(kernel, dims), out_shape=jax.ShapeDtypeS...  96.5 us

profile of v1, /device:TPU:0, one launch (start us, length us, event | category | flops | bytes accessed | tf_op | source)
XLA Modules:
  0.0 97.9 jit_solution(15505778541585193711)
XLA Ops:
  0.0 96.5 %decode_step.1 = bf16[1,5120]{1,0:T(2,128)(2,1)} custom-call(bf16[2,64,2,64,4,2,128]{6,5,4,3,2,1,0:T(2,128)(2,1)} %bitcast.1, s32[1,8,32]{2,1,0:T(8,128)} %pidx.1, bf16[1,5120]{1,0:T(2,128)(2,1)} %hid.1, bf16[2,5120]{1,0:T(2,128)(2,1)} %na.1, bf16[2,5120]{1,0:T(2,128)(2,1)} %nm.1, f32[2,128]{1,0:T(2,128)} %constant.2.clone.rope, ...), custom_call_target="tpu_custom_call" | custom-call | tf_op jit(solution)/shard_map/decode_step/pallas_call | solution.py:367
  96.5 1.4 %copy.12 = bf16[1,5120]{1,0:T(2,128)(2,1)} copy(bf16[1,5120]{1,0:T(2,128)(2,1)} %decode_step.1) | data formatting | bytes 20480

commit v2 on v1

v2 whole, which is shorter than its diff:
```python
import functools
import math

import jax
import jax.numpy as jnp
import numpy as np
from jax import lax
from jax.experimental import pallas as pl
from jax.experimental.pallas import tpu as pltpu
from jax.sharding import PartitionSpec as P

NORM_EPS = 1e-5
ROPE_BASE = 500000.0
NEG = -3.0e38
MESH = pl.DeviceIdType.MESH
F32 = jnp.float32
BF16 = jnp.bfloat16

N_DEV = 8
RING = 7
STEP = 256
HEADS_PER_GROUP = 4
SCORE_PAGES = 32
VALUE_PAGES = 32


def rope_table(position, head_dim):
    half = head_dim // 2
    freq = ROPE_BASE ** (-np.arange(half, dtype=np.float64) * 2.0 / head_dim)
    angle = position * freq
    cos = np.concatenate([np.cos(angle), np.cos(angle)])
    sin = np.concatenate([-np.sin(angle), np.sin(angle)])
    return np.stack([cos, sin]).astype(np.float32)


def kernel(dims, kv, pidx, hid, na, nm, rope, wqkv, wout, wgu, wdn, o,
           ring, k_b, v_b, dn_b, s_b,
           hid_v, na_v, nm_v, pidx_v, rope_v, x0, xf, xm, qbuf, psend, precv,
           abuf, mbuf, mrecv, maskx, mrow, snew, vnew_b,
           sm_sem, ring_sem, k_sem, v_sem, dn_sem,
           x0_s, x0_r, mk_s, mk_r, q_s, q_r, p_s, p_r, a_s, a_r, xm_s, xm_r, xf_s, xf_r, m_s, m_r):
    layers, pages, page_len, kv_heads, head_dim, rep_q, width, ffn, steps = dims
    per = HEADS_PER_GROUP
    groups = kv_heads // per
    tiles = page_len * per // 128
    slice_w = width // N_DEV
    q_w = rep_q * head_dim
    rows = rep_q * N_DEV
    scale2 = float(head_dim ** -0.5 * math.log2(math.e))

    me = lax.axis_index('pool')
    rep = lax.axis_index('replica')
    b0 = lax.rem(me, 2)
    b1 = lax.rem(me // 2, 2)
    b2 = me // 4

    def peer(k):
        return lax.rem(b0 + k % 2, 2) + 2 * lax.rem(b1 + (k // 2) % 2, 2) + 4 * lax.rem(b2 + k // 4, 2)

    def group_of(kx):
        return lax.rem(b2 + kx, 2)

    n_wq, n_wo = -(-(q_w + 2 * head_dim) // STEP), -(-slice_w // STEP)
    per_layer = n_wq + n_wo + 2 * steps

    def remote(src, dst, ssem, rsem, k):
        return pltpu.make_async_remote_copy(src_ref=src, dst_ref=dst, send_sem=ssem, recv_sem=rsem,
                                            device_id=(rep, peer(k)), device_id_type=MESH)

    FAR_FIRST = (6, 7, 4, 5, 2, 3, 1)

    def my_cols(ref, w):
        return ref.at[:, pl.ds(pl.multiple_of(me * w, 128), w)]

    def ring_slot(l, j):
        return lax.rem(l * per_layer + j, RING)

    def ring_copies(l, j):
        slot = ring_slot(l, j)

        def copy(i, src, off, w, at):
            return pltpu.make_async_copy(src.at[l, :, pl.ds(pl.multiple_of(off, 128), w)],
                                         ring.at[slot, :, pl.ds(at, w)], ring_sem.at[slot, i])

        if j < n_wq:
            lo, hi = j * STEP, (j + 1) * STEP
            parts, base = [], 0
            for off, w in ((me * q_w, q_w), (width + me * head_dim, head_dim),
                           (width + (kv_heads + me) * head_dim, head_dim)):
                x, y = max(lo, base), min(hi, base + w)
                if x < y:
                    parts.append((wqkv, off + x - base, y - x, x - lo))
                base += w
            return [copy(i, *p) for i, p in enumerate(parts)]
        if j < n_wq + n_wo:
            lo = (j - n_wq) * STEP
            return [copy(0, wout, me * slice_w + lo, min(STEP, slice_w - lo), 0)]
        s, part = divmod(j - n_wq - n_wo, 2)
        return [copy(0, wgu, part * ffn + ffn_base(me) + s * STEP, STEP, 0)]

    def refill(l, j):
        if j + RING < per_layer:
            start(ring_copies(l, j + RING))

    def kv_copies(l, which, buf, sem):
        return [pltpu.make_async_copy(kv.at[l, :, which, :, p], buf.at[p], sem.at[p]) for p in range(groups)]

    def ffn_base(dev):
        return 128 * ((dev * (ffn // 128)) // N_DEV)

    def dn_copies(l, s):
        return [pltpu.make_async_copy(
            wdn.at[l, pl.ds(pl.multiple_of(ffn_base(j) + s * STEP, 128), STEP),
                   pl.ds(pl.multiple_of(me * slice_w, 128), slice_w)],
            dn_b.at[s, pl.ds(j * STEP, STEP)], dn_sem.at[s, j]) for j in range(N_DEV)]

    def start(cps):
        for c in cps:
            c.start()

    def wait(cps):
        for c in cps:
            c.wait()

    small = [pltpu.make_async_copy(a, b, sm_sem.at[i]) for i, (a, b) in enumerate(
        ((hid, hid_v), (pidx.at[0], pidx_v), (na, na_v), (nm, nm_v), (rope, rope_v)))]
    start(small)
    for j in range(n_wq):
        start(ring_copies(0, j))

    barrier = pltpu.get_barrier_semaphore()
    for k in range(1, N_DEV):
        pl.semaphore_signal(barrier, inc=1, device_id=(rep, peer(k)), device_id_type=MESH)
    wait(small)
    x0[me] = hid_v[...].astype(F32)
    lane = lax.broadcasted_iota(jnp.int32, (N_DEV, 128), 1)
    idx = pidx_v[...]
    hit = lane < 0
    for j in range(idx.shape[1]):
        hit = jnp.logical_or(hit, idx[:, j:j + 1] == lane)
    hitf = jnp.where(hit, 1.0, 0.0).astype(F32)
    for owner in range(N_DEV):
        psend[owner, 0] = jnp.broadcast_to(hitf[owner:owner + 1, :], (N_DEV, 128))
    pl.semaphore_wait(barrier, N_DEV - 1)
    x0_cps = [remote(x0.at[me], x0.at[me], x0_s.at[k], x0_r.at[k], k) for k in FAR_FIRST]
    start(x0_cps)
    mk_cps = [remote(psend.at[peer(k), 0], mrecv.at[me], mk_s.at[k], mk_r.at[k], k) for k in FAR_FIRST]
    start(mk_cps)
    mrecv[me] = psend[me, 0]
    start(kv_copies(0, 0, k_b, k_sem))
    start(kv_copies(0, 1, v_b, v_sem))
    wait(x0_cps)
    sub8 = lax.broadcasted_iota(jnp.int32, (N_DEV, width), 0)
    xin = jnp.zeros((N_DEV, width), F32)
    for j in range(N_DEV):
        xin = jnp.where(sub8 == j, jnp.broadcast_to(x0[j], (N_DEV, width)), xin)
    xf[...] = xin.astype(BF16)

    head_lane = lax.rem(lax.broadcasted_iota(jnp.int32, (rows, 128), 1), per)
    grp = lax.broadcasted_iota(jnp.int32, (N_DEV, 128), 1) // 16
    low8 = lax.rem(lax.broadcasted_iota(jnp.int32, (N_DEV, 128), 1), 16) < 8

    def norm(x, gains, l):
        g = jnp.where(l == 0, gains[0:1, :].astype(F32), gains[1:2, :].astype(F32))
        inv = lax.rsqrt(jnp.sum(x * x, axis=-1, keepdims=True) / width + NORM_EPS)
        return (x * inv * g).astype(BF16)

    def layer(l, carry):
        h = norm(xf[...].astype(F32), na_v[...], l)
        us = []
        n_q = -(-q_w // STEP)
        for j in range(n_q):
            wait(ring_copies(l, j))
        for j in range(n_q):
            us.append(jnp.dot(h, ring[ring_slot(l, j)], preferred_element_type=F32))
        u = jnp.concatenate(us, axis=1).astype(BF16).astype(F32)
        cos = rope_v[0:1, :]
        sin = rope_v[1:2, :]

        def rot(v):
            return (v * cos + pltpu.roll(v, head_dim // 2, 1) * sin).astype(BF16)

        qs = [rot(u[:, g * head_dim:(g + 1) * head_dim]).astype(F32) for g in range(rep_q)]
        qbuf[me] = jnp.concatenate(qs, axis=0).astype(BF16)
        q_cps = {k: remote(qbuf.at[me], qbuf.at[me], q_s.at[k], q_r.at[k], k) for k in range(1, N_DEV)}
        start([q_cps[k] for k in FAR_FIRST])

        for j in range(n_q, n_wq):
            wait(ring_copies(l, j))
            w = min(STEP, q_w + 2 * head_dim - j * STEP)
            more = jnp.dot(h, ring[ring_slot(l, j), :, 0:w], preferred_element_type=F32)
            u = jnp.concatenate([u, more.astype(BF16).astype(F32)], axis=1)

        @pl.when(l == 0)
        def _():
            for j in range(n_wq, RING):
                start(ring_copies(0, j))

        for j in range(n_wq):
            refill(l, j)
        for s in range(steps):
            start(dn_copies(l, s))
        kn = rot(u[:, q_w:q_w + head_dim]).astype(F32)
        vnew_b[...] = u[:, q_w + head_dim:]
        for g in range(rep_q):
            snew[g] = jnp.broadcast_to(jnp.sum(qs[g] * kn, axis=-1, keepdims=True), (N_DEV, 128))

        @pl.when(l == 0)
        def _():
            wait(mk_cps)
            sub = lax.broadcasted_iota(jnp.int32, (N_DEV, 128), 0)
            mk = jnp.zeros((N_DEV, 128), F32)
            for r in range(N_DEV):
                mk = jnp.where(sub == r, mrecv[r], mk)
            for p in range(pages):
                maskx[p] = jnp.broadcast_to(mk[:, p:p + 1], (N_DEV, 128))

        wait(kv_copies(l, 0, k_b, k_sem))
        flat = SCORE_PAGES * page_len * per
        for kx in range(groups):
            for k in range(per * kx, per * (kx + 1)):
                if k:
                    q_cps[k].wait()
            p = group_of(kx)
            q_all = jnp.concatenate([qbuf[per * p + i] for i in range(per)], axis=0)

            def score_body(c, mx, p=p, q_all=q_all, kx=kx):
                kt = k_b[p, pl.ds(c * SCORE_PAGES, SCORE_PAGES)].reshape(flat, head_dim)
                s = lax.dot_general(q_all, kt, (((1,), (1,)), ((), ())), preferred_element_type=F32)
                for i in range(SCORE_PAGES):
                    keep = maskx[c * SCORE_PAGES + i] > 0.5
                    keep = jnp.concatenate([keep] * rep_q, axis=0)
                    for t in range(i * tiles, (i + 1) * tiles):
                        st = s[:, t * 128:(t + 1) * 128]
                        sp = st[(per - 1) * rows:]
                        for hh in range(per - 2, -1, -1):
                            sp = jnp.where(head_lane == hh, st[hh * rows:(hh + 1) * rows], sp)
                        sp = jnp.where(keep, sp, NEG)
                        s_b[kx, c * (SCORE_PAGES * tiles) + t] = sp
                        mx = jnp.maximum(mx, sp)
                return mx

            mx = lax.fori_loop(0, pages // SCORE_PAGES, score_body, jnp.full((rows, 128), NEG, F32))
            m = jnp.zeros((rows, 128), F32)
            for hh in range(per):
                m = jnp.where(head_lane == hh, jnp.max(jnp.where(head_lane == hh, mx, NEG), axis=-1, keepdims=True), m)
            mrow[kx] = m

        @pl.when(l + 1 < layers)
        def _():
            start(kv_copies(l + 1, 0, k_b, k_sem))

        wait(kv_copies(l, 1, v_b, v_sem))
        p_cps = {k: remote(psend.at[peer(k)], precv.at[me], p_s.at[k], p_r.at[k], k) for k in range(1, N_DEV)}
        for kx in reversed(range(groups)):
            p = group_of(kx)
            m = mrow[kx]

            def value_body(c, carry, p=p, m=m, kx=kx):
                acc, den = carry
                pieces = []
                for t in range(VALUE_PAGES * tiles):
                    e = jnp.exp2((s_b[kx, c * (VALUE_PAGES * tiles) + t] - m) * scale2)
                    den = den + e
                    pieces.append(jnp.concatenate([jnp.where(head_lane == hh, e, 0.0) for hh in range(per)], axis=0).astype(BF16))
                vt = v_b[p, pl.ds(c * VALUE_PAGES, VALUE_PAGES)].reshape(VALUE_PAGES * page_len * per, head_dim)
                acc = acc + jnp.dot(jnp.concatenate(pieces, axis=1), vt, preferred_element_type=F32)
                return acc, den

            acc, den = lax.fori_loop(0, pages // VALUE_PAGES, value_body,
                                     (jnp.zeros((per * rows, head_dim), F32), jnp.zeros((rows, 128), F32)))
            for hh in range(per):
                l_h = jnp.sum(jnp.where(head_lane == hh, den, 0.0), axis=-1, keepdims=True)
                m_h = jnp.max(jnp.where(head_lane == hh, m, NEG), axis=-1, keepdims=True)
                stat = jnp.zeros((N_DEV, 128), F32)
                for g in range(rep_q):
                    rs = slice(g * N_DEV, (g + 1) * N_DEV)
                    psend[per * p + hh, g] = acc[hh * rows + g * N_DEV:hh * rows + (g + 1) * N_DEV]
                    stat = jnp.where(grp == g, jnp.where(low8, m_h[rs], l_h[rs]), stat)
                psend[per * p + hh, rep_q] = stat
            for k in range(per * (kx + 1) - 1, per * kx - 1, -1):
                if k:
                    p_cps[k].start()
        precv[me] = psend[me]

        @pl.when(l + 1 < layers)
        def _():
            start(kv_copies(l + 1, 1, v_b, v_sem))

        wait([p_cps[k] for k in FAR_FIRST])
        stats = [precv[j, rep_q] for j in range(N_DEV)]
        heads_out = []
        for g in range(rep_q):
            ms = [jnp.broadcast_to(st[:, 16 * g:16 * g + 1], (N_DEV, 128)) for st in stats]
            ls = [jnp.broadcast_to(st[:, 16 * g + 8:16 * g + 9], (N_DEV, 128)) for st in stats]
            sn = snew[g]
            top = sn
            for mj in ms:
                top = jnp.maximum(top, mj)
            e_new = jnp.exp2((sn - top) * scale2)
            den = e_new
            num = jnp.zeros((N_DEV, head_dim), F32)
            for j in range(N_DEV):
                w = jnp.exp2((ms[j] - top) * scale2)
                den = den + w * ls[j]
                num = num + w * precv[j, g]
            p_new = (e_new / den).astype(BF16).astype(F32)
            heads_out.append(num / den + p_new * vnew_b[...])
        my_cols(abuf, q_w)[...] = jnp.concatenate(heads_out, axis=1).astype(BF16)
        a_cps = {k: remote(my_cols(abuf, q_w), my_cols(abuf, q_w), a_s.at[k], a_r.at[k], k) for k in range(1, N_DEV)}
        start([a_cps[k] for k in FAR_FIRST])

        for j in range(n_wo):
            wait(ring_copies(l, n_wq + j))
        projs = [None] * n_wo
        xm_cps = []

        def out_cols(j):
            return pl.ds(pl.multiple_of(me * slice_w + j * STEP, 128), min(STEP, slice_w - j * STEP))

        half = width // 2
        for kx in range(2):
            wait([a_cps[k] for k in range(4 * kx, 4 * kx + 4) if k])
            at = pl.ds(pl.multiple_of(group_of(kx) * half, 128), half)
            for j in range(n_wo):
                w = min(STEP, slice_w - j * STEP)
                d = jnp.dot(abuf[:, at], ring[ring_slot(l, n_wq + j), at, 0:w], preferred_element_type=F32)
                projs[j] = d if kx == 0 else projs[j] + d
                if kx:
                    cols = out_cols(j)
                    xm[:, cols] = (xf[:, cols].astype(F32) + projs[j]).astype(BF16)
                    cps = [remote(xm.at[:, cols], xm.at[:, cols], xm_s.at[j, k], xm_r.at[j, k], k) for k in FAR_FIRST]
                    start(cps)
                    xm_cps += cps
        for j in range(n_wo):
            refill(l, n_wq + j)
        wait(xm_cps)

        h2 = norm(xm[...].astype(F32), nm_v[...], l)
        mlane = lax.broadcasted_iota(jnp.int32, (N_DEV, STEP), 1)

        def m_cps(s):
            cols = pl.ds(pl.multiple_of(me * STEP, 128), STEP)
            return [remote(mbuf.at[s, :, cols], mbuf.at[s, :, cols], m_s.at[s, k], m_r.at[s, k], k) for k in FAR_FIRST]

        def activate(s, gate, up):
            gate = gate.astype(BF16).astype(F32)
            act = gate / (1.0 + jnp.exp(-gate)) * up.astype(BF16).astype(F32)
            if s == 0:
                act = jnp.where(jnp.logical_and(b0 == 1, mlane < 128), 0.0, act)
            mbuf[s, :, pl.ds(pl.multiple_of(me * STEP, 128), STEP)] = act.astype(BF16)

        before = None
        for s in range(steps):
            j = n_wq + n_wo + 2 * s
            wait(ring_copies(l, j))
            wait(ring_copies(l, j + 1))
            gate = jnp.dot(h2, ring[ring_slot(l, j)], preferred_element_type=F32)
            up = jnp.dot(h2, ring[ring_slot(l, j + 1)], preferred_element_type=F32)
            if s:
                activate(s - 1, *before)
                start(m_cps(s - 1))
            before = (gate, up)
            refill(l, j)
            refill(l, j + 1)
        activate(steps - 1, *before)
        start(m_cps(steps - 1))

        @pl.when(l + 1 < layers)
        def _():
            for j in range(n_wq):
                start(ring_copies(l + 1, j))

        def down_step(s):
            wait(dn_copies(l, s))
            wait(m_cps(s))

        def down_body(i, acc):
            down_step(2 * i)
            down_step(2 * i + 1)
            acc = (acc + jnp.dot(mbuf[2 * i], dn_b[2 * i], preferred_element_type=F32)
                   + jnp.dot(mbuf[2 * i + 1], dn_b[2 * i + 1], preferred_element_type=F32))
            return acc

        acc = lax.fori_loop(0, steps // 2, down_body, jnp.zeros((N_DEV, slice_w), F32))
        tail = steps - steps % 2
        for st in range(tail, steps):
            down_step(st)
        xf_cps, news = [], []
        for j in range(n_wo):
            lo, hi = j * STEP, min((j + 1) * STEP, slice_w)
            part = acc[:, lo:hi]
            for st in range(tail, steps):
                part = part + jnp.dot(mbuf[st], dn_b[st, :, lo:hi], preferred_element_type=F32)
            cols = out_cols(j)
            new = (xm[:, cols].astype(F32) + part).astype(BF16)
            news.append(new)
            cps = [remote(xf.at[:, cols], xf.at[:, cols], xf_s.at[j, k], xf_r.at[j, k], k) for k in FAR_FIRST]
            xf_cps += cps

            @pl.when(l + 1 < layers)
            def _(new=new, cols=cols, cps=cps):
                xf[:, cols] = new
                start(cps)

        @pl.when(l + 1 < layers)
        def _():
            for j in range(n_wq, RING):
                start(ring_copies(l + 1, j))
            wait(xf_cps)

        @pl.when(l + 1 == layers)
        def _():
            row = jnp.concatenate(news, axis=1).astype(F32)
            for r in range(N_DEV):
                x0[r, :, slice_w:2 * slice_w] = row[r:r + 1]
            cps = [remote(x0.at[peer(k), :, pl.ds(slice_w, slice_w)], x0.at[me, :, pl.ds(0, slice_w)],
                          x0_s.at[k], x0_r.at[k], k) for k in FAR_FIRST]
            start(cps)
            x0[me, :, 0:slice_w] = x0[me, :, slice_w:2 * slice_w]
            wait(cps)
            for j in range(N_DEV):
                o[:, j * slice_w:(j + 1) * slice_w] = x0[j, :, 0:slice_w].astype(BF16)
        return carry

    lax.fori_loop(0, layers, layer, 0)


def solution(mesh):
    def device_fn(kv_pool, page_idx, hidden, norm_attn, norm_mlp, w_qkv, w_out, w_gate_up, w_down):
        layers, pages, _, page_len, kv_heads, head_dim = kv_pool.shape
        group, take = page_idx.shape[1:]
        width = hidden.shape[1]
        ffn = w_down.shape[1]
        rep_q = (w_qkv.shape[2] - 2 * kv_heads * head_dim) // head_dim // kv_heads
        rows = rep_q * group
        slice_w = width // group
        q_w = rep_q * head_dim
        steps = -(-(-(-(ffn // 128) // group)) // (STEP // 128))
        position = float(group * take * page_len)
        n_out = -(-slice_w // STEP)
        rope = jnp.asarray(rope_table(position, head_dim))
        groups = kv_heads // HEADS_PER_GROUP
        kv = kv_pool.reshape(layers, pages, 2, page_len, groups, HEADS_PER_GROUP, head_dim)
        dims = (layers, pages, page_len, kv_heads, head_dim, rep_q, width, ffn, steps)
        dma = pltpu.SemaphoreType.DMA
        any_spec = pl.BlockSpec(memory_space=pl.ANY)
        tiles = page_len * HEADS_PER_GROUP // 128
        return pl.pallas_call(
            functools.partial(kernel, dims),
            out_shape=jax.ShapeDtypeStruct((1, width), BF16),
            in_specs=[any_spec] * 10,
            out_specs=pl.BlockSpec(memory_space=pltpu.VMEM),
            scratch_shapes=[
                pltpu.VMEM((RING, width, STEP), BF16),
                pltpu.VMEM((groups, pages, page_len, HEADS_PER_GROUP, head_dim), BF16),
                pltpu.VMEM((groups, pages, page_len, HEADS_PER_GROUP, head_dim), BF16),
                pltpu.VMEM((steps, group * STEP, slice_w), BF16),
                pltpu.VMEM((groups, pages * tiles, rows, 128), F32),
                pltpu.VMEM((1, width), BF16),
                pltpu.VMEM((layers, width), BF16),
                pltpu.VMEM((layers, width), BF16),
                pltpu.VMEM((group, take), jnp.int32),
                pltpu.VMEM((2, head_dim), F32),
                pltpu.VMEM((group, 1, width), F32),
                pltpu.VMEM((group, width), BF16),
                pltpu.VMEM((group, width), BF16),
                pltpu.VMEM((group, rows, head_dim), BF16),
                pltpu.VMEM((group, rep_q + 1, group, 128), F32),
                pltpu.VMEM((group, rep_q + 1, group, 128), F32),
                pltpu.VMEM((group, width), BF16),
                pltpu.VMEM((steps, group, group * STEP), BF16),
                pltpu.VMEM((group, group, 128), F32),
                pltpu.VMEM((pages, group, 128), F32),
                pltpu.VMEM((groups, rows, 128), F32),
                pltpu.VMEM((rep_q, group, 128), F32),
                pltpu.VMEM((group, head_dim), F32),
                dma((5,)), dma((RING, 2)), dma((groups,)), dma((groups,)), dma((steps, group)),
            ] + [dma((group,))] * 10 + [dma((n_out, group))] * 4 + [dma((steps, group))] * 2,
            compiler_params=pltpu.CompilerParams(
                collective_id=0, has_side_effects=True, vmem_limit_bytes=67_043_328),
            name="decode_step",
        )(kv, page_idx, hidden, norm_attn, norm_mlp, rope, w_qkv, w_out, w_gate_up, w_down)

    row_spec = P(('replica', 'pool'))
    in_specs = (P(None, ('replica', 'pool')), row_spec, row_spec, P(), P(), P(), P(), P(), P())
    return jax.shard_map(device_fn, mesh=mesh, in_specs=in_specs, out_specs=row_spec, check_vma=False)
```

time: 98.1 us -> 92.5 us (0.943)
  Pallas kernels: 96.5 us -> 91 us
    pallas_call x1, Pallas kernels: 96.5 us -> 91 us  [device_fn(): pl.pallas_call(functools.partial(kernel, dims), out_shape=jax.ShapeDtypeS...]
where the time goes in v2:
time: 92.5 us; the launch traced here: 92.4 us
  Pallas kernels  91 us (98%)
  local copies, waits for them, and re-layouts  1.36 us (1%)
    pallas_call x1, Pallas kernels, device_fn(): pl.pallas_call(functools.partial(kernel, dims), out_shape=jax.ShapeDtypeS...  91 us

profile of v2, /device:TPU:0, one launch (start us, length us, event | category | flops | bytes accessed | tf_op | source)
XLA Modules:
  0.0 92.4 jit_solution(12894642650771912057)
XLA Ops:
  0.0 91.0 %decode_step.1 = bf16[1,5120]{1,0:T(2,128)(2,1)} custom-call(bf16[2,64,2,64,2,4,128]{6,5,4,3,2,1,0:T(4,128)(2,1)} %bitcast.1, s32[1,8,32]{2,1,0:T(8,128)} %pidx.1, bf16[1,5120]{1,0:T(2,128)(2,1)} %hid.1, bf16[2,5120]{1,0:T(2,128)(2,1)} %na.1, bf16[2,5120]{1,0:T(2,128)(2,1)} %nm.1, f32[2,128]{1,0:T(2,128)} %constant.2.clone.rope, ...), custom_call_target="tpu_custom_call" | custom-call | tf_op jit(solution)/shard_map/decode_step/pallas_call | solution.py:449
  91.0 1.4 %copy.12 = bf16[1,5120]{1,0:T(2,128)(2,1)} copy(bf16[1,5120]{1,0:T(2,128)(2,1)} %decode_step.1) | data formatting | bytes 20480

commit v3 on v2

--- a/solution.py
+++ b/solution.py
@@ -17,11 +17,12 @@
 BF16 = jnp.bfloat16
 
 N_DEV = 8
-RING = 7
+RING = 8
 STEP = 256
 HEADS_PER_GROUP = 4
 SCORE_PAGES = 32
 VALUE_PAGES = 32
+DOT_PAGES = 8
 
 
 def rope_table(position, head_dim):
@@ -213,10 +214,10 @@
             for r in range(N_DEV):
                 mk = jnp.where(sub == r, mrecv[r], mk)
             for p in range(pages):
-                maskx[p] = jnp.broadcast_to(mk[:, p:p + 1], (N_DEV, 128))
+                maskx[p] = jnp.broadcast_to(mk[:, p:p + 1], (N_DEV, 128)).astype(BF16)
 
         wait(kv_copies(l, 0, k_b, k_sem))
-        flat = SCORE_PAGES * page_len * per
+        flat = DOT_PAGES * page_len * per
         for kx in range(groups):
             for k in range(per * kx, per * (kx + 1)):
                 if k:
@@ -225,13 +226,15 @@
             q_all = jnp.concatenate([qbuf[per * p + i] for i in range(per)], axis=0)
 
             def score_body(c, mx, p=p, q_all=q_all, kx=kx):
-                kt = k_b[p, pl.ds(c * SCORE_PAGES, SCORE_PAGES)].reshape(flat, head_dim)
-                s = lax.dot_general(q_all, kt, (((1,), (1,)), ((), ())), preferred_element_type=F32)
                 for i in range(SCORE_PAGES):
-                    keep = maskx[c * SCORE_PAGES + i] > 0.5
+                    if i % DOT_PAGES == 0:
+                        kt = k_b[p, pl.ds(c * SCORE_PAGES + i, DOT_PAGES)].reshape(flat, head_dim)
+                        s = lax.dot_general(q_all, kt, (((1,), (1,)), ((), ())), preferred_element_type=F32)
+                    keep = maskx[c * SCORE_PAGES + i].astype(F32) > 0.5
                     keep = jnp.concatenate([keep] * rep_q, axis=0)
                     for t in range(i * tiles, (i + 1) * tiles):
-                        st = s[:, t * 128:(t + 1) * 128]
+                        lo = (t % (DOT_PAGES * tiles)) * 128
+                        st = s[:, lo:lo + 128]
                         sp = st[(per - 1) * rows:]
                         for hh in range(per - 2, -1, -1):
                             sp = jnp.where(head_lane == hh, st[hh * rows:(hh + 1) * rows], sp)
@@ -258,13 +261,14 @@
 
             def value_body(c, carry, p=p, m=m, kx=kx):
                 acc, den = carry
-                pieces = []
-                for t in range(VALUE_PAGES * tiles):
-                    e = jnp.exp2((s_b[kx, c * (VALUE_PAGES * tiles) + t] - m) * scale2)
-                    den = den + e
-                    pieces.append(jnp.concatenate([jnp.where(head_lane == hh, e, 0.0) for hh in range(per)], axis=0).astype(BF16))
-                vt = v_b[p, pl.ds(c * VALUE_PAGES, VALUE_PAGES)].reshape(VALUE_PAGES * page_len * per, head_dim)
-                acc = acc + jnp.dot(jnp.concatenate(pieces, axis=1), vt, preferred_element_type=F32)
+                for d in range(0, VALUE_PAGES, DOT_PAGES):
+                    pieces = []
+                    for t in range(d * tiles, (d + DOT_PAGES) * tiles):
+                        e = jnp.exp2((s_b[kx, c * (VALUE_PAGES * tiles) + t] - m) * scale2)
+                        den = den + e
+                        pieces.append(jnp.concatenate([jnp.where(head_lane == hh, e, 0.0) for hh in range(per)], axis=0).astype(BF16))
+                    vt = v_b[p, pl.ds(c * VALUE_PAGES + d, DOT_PAGES)].reshape(flat, head_dim)
+                    acc = acc + jnp.dot(jnp.concatenate(pieces, axis=1), vt, preferred_element_type=F32)
                 return acc, den
 
             acc, den = lax.fori_loop(0, pages // VALUE_PAGES, value_body,
@@ -471,7 +475,7 @@
                 pltpu.VMEM((group, width), BF16),
                 pltpu.VMEM((steps, group, group * STEP), BF16),
                 pltpu.VMEM((group, group, 128), F32),
-                pltpu.VMEM((pages, group, 128), F32),
+                pltpu.VMEM((pages, group, 128), BF16),
                 pltpu.VMEM((groups, rows, 128), F32),
                 pltpu.VMEM((rep_q, group, 128), F32),
                 pltpu.VMEM((group, head_dim), F32),

time: 92.5 us -> 91 us (0.984)
  Pallas kernels: 91 us -> 89.5 us
    pallas_call x1, Pallas kernels: 91 us -> 89.5 us  [device_fn(): pl.pallas_call(functools.partial(kernel, dims), out_shape=jax.ShapeDtypeS...]
where the time goes in v3:
time: 91 us; the launch traced here: 90.9 us
  Pallas kernels  89.5 us (98%)
  local copies, waits for them, and re-layouts  1.36 us (1%)
    pallas_call x1, Pallas kernels, device_fn(): pl.pallas_call(functools.partial(kernel, dims), out_shape=jax.ShapeDtypeS...  89.5 us

profile of v3, /device:TPU:0, one launch (start us, length us, event | category | flops | bytes accessed | tf_op | source)
XLA Modules:
  0.0 90.9 jit_solution(7683118050734028773)
XLA Ops:
  0.0 89.5 %decode_step.1 = bf16[1,5120]{1,0:T(2,128)(2,1)} custom-call(bf16[2,64,2,64,2,4,128]{6,5,4,3,2,1,0:T(4,128)(2,1)} %bitcast.1, s32[1,8,32]{2,1,0:T(8,128)} %pidx.1, bf16[1,5120]{1,0:T(2,128)(2,1)} %hid.1, bf16[2,5120]{1,0:T(2,128)(2,1)} %na.1, bf16[2,5120]{1,0:T(2,128)(2,1)} %nm.1, f32[2,128]{1,0:T(2,128)} %constant.2.clone.rope, ...), custom_call_target="tpu_custom_call" | custom-call | tf_op jit(solution)/shard_map/decode_step/pallas_call | solution.py:453
  89.5 1.4 %copy.12 = bf16[1,5120]{1,0:T(2,128)(2,1)} copy(bf16[1,5120]{1,0:T(2,128)(2,1)} %decode_step.1) | data formatting | bytes 20480
